TPU v7x, 128 devices: a whole 4x4x4 slice. The times are simulated.
128 devices in a mesh: seq: 16 (over y, x_hi, core), head: 8 (over z, x_lo).
Axes of the slice: x: 4 (x_hi: 2, x_lo: 2; x = x_hi * 2 + x_lo), y: 4, z: 4, core: 2. Of those that a mesh axis runs over, the one named last changes fastest.
Arguments:
- d_bytes: bfloat16 [4096, 8192], P('seq', 'head'), may hold values from -6 to 6
- owner_groups: int32 [16, 16], replicated, may hold values from 0 to 255, as said below
- block_order: int32 [16], replicated, may hold values from 0 to 15, each once
- y_in: bfloat16 [4096, 4096], P('seq'), may hold values from -0.29882812 to 0.29882812
- w_proj: bfloat16 [4096, 8192], P('seq', 'head'), may hold values from -0.0625 to 0.0625
- w_out: bfloat16 [2048, 4096], P('head', 'seq'), may hold values from -0.125 to 0.125
- queries: bfloat16 [4096, 2048], P('seq', 'head'), may hold values from -24 to 24
- keys: bfloat16 [4096, 2048], P('seq', 'head'), may hold values from -24 to 24
- values: bfloat16 [4096, 2048], P('seq', 'head'), may hold values from -6 to 6
- attn_out: bfloat16 [4096, 2048], P('seq', 'head'), may hold values from -0.59765625 to 0.59765625
Outputs:
- layer_grad: bfloat16 [4096, 4096], P('seq', 'head')
- grad_proj: bfloat16 [4096, 8192], P('seq', 'head')
- grad_out: bfloat16 [2048, 4096], P('head', 'seq')
- grad_queries: bfloat16 [4096, 2048], P('seq', 'head')
- grad_keys: bfloat16 [4096, 2048], P('seq', 'head')
- grad_values: bfloat16 [4096, 2048], P('seq', 'head')
Inputs may be any that keep to these rules, and one draw needn't show every extreme that they name: `owner_groups`: row o lists the patch groups held by owner o; it holds exactly one group of every seq shard (group g covers patches g * 16 to g * 16 + 15, shard g // 16), and every group appears once. `block_order`: A permutation.
All inputs are finite; a program needn't handle non-finite values.
Results may differ from a plain program's by a relative error of at most 0.03.
Values may be sent and summed in bfloat16 or wider, within the bound.
No kernel may reach another device: no remote copies, remote signals or barrier semaphores. Data moves between devices by JAX's collectives and lax.ppermute only.
A program may use at most 128 MiB of HBM per device.

v0:
```python
import math
import jax
import jax.numpy as jnp
from jax import lax
from jax.sharding import PartitionSpec as P

HEAD_DIM = 128


def in_blocks(shard, dim, peers):
    before, after = (shard.shape[:dim], shard.shape[dim + 1 :])
    return jnp.moveaxis(shard.reshape(*before, peers, -1, *after), dim, 0)


def summed_on_arrival(shard, axis, dim):
    pieces = in_blocks(shard, dim, lax.axis_size(axis))
    arrived = lax.all_to_all(pieces, axis, split_axis=0, concat_axis=0, tiled=True)
    return arrived.astype(jnp.float32).sum(axis=0)


def in_order(pieces, dim):
    shape = list(pieces.shape[1:])
    shape[dim] *= pieces.shape[0]
    return jnp.moveaxis(pieces, 0, dim).reshape(shape)


def from_everyone(shard, axis):
    peers = lax.axis_size(axis)
    return lax.all_to_all(
        jnp.broadcast_to(shard[None], (peers, *shard.shape)), axis, 0, 0, tiled=True
    )


def gathered_copies(shard, axis, dim):
    return in_order(from_everyone(shard, axis), dim)


def in_one_piece(arrays, axis, dim, along):
    both = jnp.concatenate(arrays, axis=along)
    filled, at, gathered = (lax.all_gather(both, axis, axis=dim, tiled=True), 0, [])
    for a in arrays:
        gathered.append(lax.slice_in_dim(filled, at, at + a.shape[along], axis=along))
        at += a.shape[along]
    return tuple(gathered)


def sent_together(arrays, axis, dim, along):
    ends, at = ([], 0)
    for a in arrays[:-1]:
        at += a.shape[along]
        ends.append(at)
    both = jnp.concatenate(arrays, axis=along)
    return tuple(
        jnp.split(lax.psum_scatter(both, axis, scatter_dimension=dim, tiled=True), ends, axis=along)
    )


def body(d_bytes, owner_groups, block_order, y_in, w_proj, w_out, queries, keys, values, attn_out):
    flt = jnp.float32
    half = jnp.bfloat16
    owners = lax.axis_size("seq")
    seq_index = lax.axis_index("seq")
    patch_dev = y_in.shape[0]
    group_rows = patch_dev // owners
    columns = d_bytes.shape[1]
    owner_ids = jnp.arange(owners, dtype=jnp.int32)
    mine = jnp.sum(jnp.where(owner_ids[:, None] == seq_index, owner_groups, 0), axis=0)
    sending = jnp.argsort(mine // owners)
    outgoing = jnp.take(d_bytes.reshape(owners, group_rows, columns), sending, axis=0)
    incoming = lax.all_to_all(outgoing, "seq", split_axis=0, concat_axis=0, tiled=True)
    landing = jnp.sum(
        jnp.where(owner_groups // owners == seq_index, owner_groups % owners, 0), axis=1
    )
    arrival = jnp.argsort(landing)
    natural = jnp.take(incoming, arrival, axis=0).reshape(patch_dev, columns)
    grad_proj = (
        lax.psum_scatter(
            lax.dot_general(
                y_in, natural, (((0,), (0,)), ((), ())), preferred_element_type=flt
            ).astype(jnp.bfloat16),
            "seq",
            scatter_dimension=0,
            tiled=True,
        )
        .astype(jnp.float32)
        .astype(half)
    )
    head_part = lax.dot_general(
        natural,
        lax.all_gather(w_proj, "seq", axis=0, tiled=True),
        (((1,), (1,)), ((), ())),
        preferred_element_type=flt,
    )
    layer_grad = summed_on_arrival(head_part.astype(jnp.bfloat16), "head", 1).astype(half)
    full_grad = gathered_copies(layer_grad, "head", 1)
    width_dev = queries.shape[1]
    attn_grad = lax.dot_general(
        full_grad,
        lax.all_gather(w_out, "seq", axis=1, tiled=True),
        (((1,), (1,)), ((), ())),
        preferred_element_type=flt,
    ).astype(half)
    out_term = lax.dot_general(
        attn_out, full_grad, (((0,), (0,)), ((), ())), preferred_element_type=flt
    )
    grad_out = summed_on_arrival(out_term.astype(jnp.bfloat16), "seq", 1).astype(half)
    heads_dev = width_dev // HEAD_DIM
    scale = 1.0 / math.sqrt(HEAD_DIM)
    query_heads = queries.reshape(patch_dev, heads_dev, HEAD_DIM)
    grad_heads = attn_grad.reshape(patch_dev, heads_dev, HEAD_DIM)
    delta = jnp.sum(
        grad_heads.astype(flt) * attn_out.reshape(patch_dev, heads_dev, HEAD_DIM).astype(flt),
        axis=2,
    ).T
    local_rows = jnp.arange(patch_dev, dtype=jnp.int32)
    my_block = jnp.sum(jnp.where(owner_ids == seq_index, block_order, 0))
    query_pos = my_block * patch_dev + local_rows
    keys_all, values_all = in_one_piece((keys, values), "seq", 0, 1)
    all_rows = keys_all.shape[0]
    block_rows = math.gcd(512, all_rows)
    block_count = all_rows // block_rows
    row_ids = jnp.arange(all_rows, dtype=jnp.int32)
    row_owner = row_ids // patch_dev
    key_pos = (
        jnp.sum(
            jnp.where(row_owner[:, None] == owner_ids[None, :], block_order[None, :], 0), axis=1
        )
        * patch_dev
        + row_ids % patch_dev
    )
    key_blocks = keys_all.reshape(block_count, block_rows, heads_dev, HEAD_DIM)
    value_blocks = values_all.reshape(block_count, block_rows, heads_dev, HEAD_DIM)
    pos_blocks = key_pos.reshape(block_count, block_rows)

    def scores_of(key_block, pos_block):
        scores = (
            jnp.einsum("qhd,khd->hqk", query_heads, key_block, preferred_element_type=flt) * scale
        )
        allowed = pos_block[None, :] <= query_pos[:, None]
        return (scores, allowed)

    def statistics(running, pieces):
        highest, totals = running
        key_block, pos_block = pieces
        scores, allowed = scores_of(key_block, pos_block)
        scores = jnp.where(allowed[None], scores, -1e30)
        new_high = jnp.maximum(highest, jnp.max(scores, axis=2))
        weights = jnp.where(allowed[None], jnp.exp(scores - new_high[:, :, None]), 0.0)
        totals = totals * jnp.exp(highest - new_high) + jnp.sum(weights, axis=2)
        return ((new_high, totals), None)

    start_stats = (
        jnp.full((heads_dev, patch_dev), -1e30, flt),
        jnp.zeros((heads_dev, patch_dev), flt),
    )
    (highest, totals), _ = lax.scan(statistics, start_stats, (key_blocks, pos_blocks))
    log_total = highest + jnp.log(totals)

    def backward(grad_query, pieces):
        key_block, value_block, pos_block = pieces
        scores, allowed = scores_of(key_block, pos_block)
        weights = jnp.where(allowed[None], jnp.exp(scores - log_total[:, :, None]), 0.0)
        grad_weights = jnp.einsum(
            "qhd,khd->hqk", grad_heads, value_block, preferred_element_type=flt
        )
        grad_scores = (weights * (grad_weights - delta[:, :, None]) * scale).astype(half)
        weights_low = weights.astype(half)
        grad_query = grad_query + jnp.einsum(
            "hqk,khd->qhd", grad_scores, key_block, preferred_element_type=flt
        )
        key_term = jnp.einsum("hqk,qhd->khd", grad_scores, query_heads, preferred_element_type=flt)
        value_term = jnp.einsum("hqk,qhd->khd", weights_low, grad_heads, preferred_element_type=flt)
        return (grad_query, (key_term, value_term))

    start_grad = jnp.zeros((patch_dev, heads_dev, HEAD_DIM), flt)
    grad_query, (key_terms, value_terms) = lax.scan(
        backward, start_grad, (key_blocks, value_blocks, pos_blocks)
    )
    key_terms = key_terms.reshape(all_rows, width_dev)
    value_terms = value_terms.reshape(all_rows, width_dev)
    grad_keys, grad_values = tuple(
        (
            part.astype(jnp.float32)
            for part in sent_together(
                (key_terms.astype(jnp.bfloat16), value_terms.astype(jnp.bfloat16)), "seq", 0, 1
            )
        )
    )
    grad_queries = grad_query.reshape(patch_dev, width_dev).astype(half)
    return (
        layer_grad,
        grad_proj,
        grad_out,
        grad_queries,
        grad_keys.astype(half),
        grad_values.astype(half),
    )


def solution(mesh):
    placed = (
        P("seq", "head"),
        P(),
        P(),
        P("seq", None),
        P("seq", "head"),
        P("head", "seq"),
        P("seq", "head"),
        P("seq", "head"),
        P("seq", "head"),
        P("seq", "head"),
    )
    return jax.shard_map(
        body,
        mesh=mesh,
        in_specs=placed,
        out_specs=(
            P("seq", "head"),
            P("seq", "head"),
            P("head", "seq"),
            P("seq", "head"),
            P("seq", "head"),
            P("seq", "head"),
        ),
        check_vma=False,
    )
```

profile of v0, /device:TPU:0, one launch (start us, length us, event | category | flops | bytes accessed | tf_op | source)
XLA Modules:
  0.0 408.7 jit_solution(1989037170501856111)
XLA Ops:
  15.2 7.1 %all-to-all-start = ((bf16[16,16,1024]{2,1,0:T(8,128)(2,1)}), bf16[16,16,1024]{2,1,0:T(8,128)(2,1)S(1)}, u32[]{:S(2)}, u32[]{:S(2)}) async-start(bf16[16,16,1024]{2,1,0:T(8,128)(2,1)} %broadcast_select_fusion.2), calls=%async_computation | async-start | bytes 1048576 | tf_op jit(solution)/shard_map/all_to_all | solution.py:70
  23.8 16.4 %all-to-all-done = bf16[16,16,1024]{2,1,0:T(8,128)(2,1)S(1)} async-done(((bf16[16,16,1024]{2,1,0:T(8,128)(2,1)}), bf16[16,16,1024]{2,1,0:T(8,128)(2,1)S(1)}, u32[]{:S(2)}, u32[]{:S(2)}) %all-to-all-start) | async-done | bytes 524320 | tf_op jit(solution)/shard_map/all_to_all | solution.py:70
  40.9 49.9 %all-gather.4.cloned.1.call-done = bf16[4096,1024]{1,0:T(8,128)(2,1)} async-done(((bf16[256,1024]{1,0:T(8,128)(2,1)}), bf16[4096,1024]{1,0:T(8,128)(2,1)}) %all-gather.4.cloned.1.call-update) | async-done | bytes 8388624 | tf_op jit(solution)/shard_map/all_gather | solution.py:90
  90.8 5.8 %convolution_convert_fusion = bf16[256,4096]{1,0:T(8,128)(2,1)S(1)} fusion(bf16[256,1024]{1,0:T(8,128)(2,1)S(1)} %bitcast.139, bf16[4096,1024]{1,0:T(8,128)(2,1)} %all-gather.4.cloned.1.call-done), kind=kOutput, calls=%fused_computation.47 | convolution fusion | flops 2148532224 | bytes 11010048 | tf_op jit(solution)/shard_map/dot_general | solution.py:88
  98.1 4.6 %all-to-all-start.1 = ((bf16[8,256,512]{2,1,0:T(8,128)(2,1)}), bf16[8,256,512]{2,1,0:T(8,128)(2,1)}, u32[]{:S(2)}, u32[]{:S(2)}) async-start(bf16[8,256,512]{2,1,0:T(8,128)(2,1)} %bitcast.135), calls=%async_computation.1 | async-start | bytes 4194304 | tf_op jit(solution)/shard_map/all_to_all | solution.py:17
  105.7 5.6 %convert_bitcast_fusion = bf16[4096,1024]{0,1:T(8,128)(2,1)} fusion(bf16[256,1024]{1,0:T(8,128)(2,1)S(1)} %bitcast.140, bf16[256,4096]{1,0:T(8,128)(2,1)S(1)} %copy-done), kind=kOutput, calls=%fused_computation.46 | convolution fusion | flops 2151677952 | bytes 11010048 | tf_op jit(solution)/shard_map/dot_general | solution.py:78
  111.3 38.1 %all-gather.6.cloned.1.call-done = bf16[4096,512]{1,0:T(8,128)(2,1)} async-done(((bf16[256,512]{1,0:T(8,128)(2,1)}), bf16[4096,512]{1,0:T(8,128)(2,1)}) %all-gather.6.cloned.1.call-update) | async-done | bytes 4194320 | tf_op jit(solution)/shard_map/all_gather | solution.py:40
  149.4 4.5 %fusion.40 = (bf16[4096,256]{1,0:T(8,128)(2,1)}, bf16[4096,256]{1,0:T(8,128)(2,1)}) fusion(bf16[4096,512]{1,0:T(8,128)(2,1)} %all-gather.6.cloned.1.call-done), kind=kLoop, calls=%fused_computation.99 | loop fusion | bytes 8388608 | tf_op jit(solution)/shard_map/slice | solution.py:42
  154.0 2.5 reshape.169
  158.3 2.0 reduce_sum.80
  161.9 4.8 %all-to-all-start.2 = ((bf16[8,256,512]{1,2,0:T(8,128)(2,1)}), bf16[8,256,512]{1,2,0:T(8,128)(2,1)S(1)}, u32[]{:S(2)}, u32[]{:S(2)}) async-start(bf16[8,256,512]{1,2,0:T(8,128)(2,1)} %broadcast_in_dim.101), calls=%async_computation.3 | async-start | bytes 4194304 | tf_op jit(solution)/shard_map/all_to_all | solution.py:29
  167.0 19.6 %while.28 = (s32[]{:T(128)}, f32[2,256]{1,0:T(2,128)S(1)}, f32[2,256]{1,0:T(2,128)S(1)}, s32[8,512]{1,0:T(8,128)}, bf16[8,512,2,128]{3,1,2,0:T(8,128)(2,1)}, /*i...) while((s32[]{:T(128)}, f32[2,256]{1,0:T(2,128)S(1)}, ...), condition=%wide.region_12.14_spmd.clone, body=%wide.region_9.13_spmd.clone.sunk | while | flops 68815616 | bytes 2918524 | solution.py:156
  186.6 4.1 reshape.170
  190.7 12.7 %all-gather.8.cloned.1.call-done = bf16[256,4096]{1,0:T(8,128)(2,1)} async-done(((bf16[256,256]{1,0:T(8,128)(2,1)}), bf16[256,4096]{1,0:T(8,128)(2,1)}) %all-gather.8.cloned.1.call-update) | async-done | bytes 2097168 | tf_op jit(solution)/shard_map/all_gather | solution.py:99
  203.4 3.1 multiply_reduce_fusion
  206.6 55.9 %while.29 = (s32[]{:T(128)}, f32[256,2,128]{0,2,1:T(8,128)S(1)}, bf16[8,512,2,128]{3,1,2,0:T(8,128)(2,1)}, bf16[8,512,2,128]{3,1,2,0:T(8,128)(2,1)}, bf16[8,512,...) while((s32[]{:T(128)}, f32[256,2,128]{0,2,1:T(8,128)S(1)}, ...), condition=%wide.region_15.17_spmd.clone, body=%wide.region_14.16_spmd.clone.sunk | while | flops 337903872 | bytes 8401075 | solution.py:176
  262.5 3.9 copy.76
  266.4 2.2 copy.75
  269.4 2.3 pad_maximum_fusion
  273.3 2.0 convolution_convert_fusion.1
  275.4 4.5 %all-to-all-start.3 = ((bf16[16,256,256]{1,2,0:T(8,128)(2,1)}), bf16[16,256,256]{1,2,0:T(8,128)(2,1)}, u32[]{:S(2)}, u32[]{:S(2)}) async-start(bf16[16,256,256]{1,2,0:T(8,128)(2,1)} %bitcast.134), calls=%async_computation.4 | async-start | bytes 4194304 | tf_op jit(solution)/shard_map/all_to_all | solution.py:17
  279.8 37.9 %reduce-scatter.3.cloned.1.call-done = bf16[256,1024]{0,1:T(8,128)(2,1)} async-done(((bf16[4096,1024]{0,1:T(8,128)(2,1)}), bf16[256,1024]{0,1:T(8,128)(2,1)}) %reduce-scatter.3.cloned.1.call-update) | async-done | bytes 524304 | tf_op jit(solution)/shard_map/reduce_scatter | solution.py:77
  317.7 2.2 copy.77
  323.3 77.2 %reduce-scatter.5.cloned.1.call-done = bf16[256,512]{1,0:T(8,128)(2,1)} async-done(((bf16[4096,512]{1,0:T(8,128)(2,1)}), bf16[256,512]{1,0:T(8,128)(2,1)}) %reduce-scatter.5.cloned.1.call-update) | async-done | bytes 262160 | tf_op jit(solution)/shard_map/reduce_scatter | solution.py:54
  (219 shorter events, 99.9 us)
Async XLA Ops:
  7.2 98.5 %copy-start = (bf16[256,4096]{1,0:T(8,128)(2,1)S(1)}, bf16[256,4096]{1,0:T(8,128)(2,1)}, u32[]{:S(2)}) copy-start(bf16[256,4096]{1,0:T(8,128)(2,1)} %param.19) | copy-start | bytes 6291460
  7.2 83.6 %all-gather.4.cloned.1.call-start = ((), (), s32[]{:S(2)}) async-start(), calls=%async_computation.6 | async-start | bytes 8912896 | tf_op jit(solution)/shard_map/all_gather | solution.py:90
  7.9 15.7 %copy-start.12 = (s32[16]{0:T(128)S(1)}, s32[16]{0:T(128)}, u32[]{:S(2)}) copy-start(s32[16]{0:T(128)} %param.18) | copy-start | bytes 196
  7.9 141.5 %all-gather.6.cloned.1.call-start = ((), (), s32[]{:S(2)}) async-start(), calls=%async_computation.8 | async-start | bytes 4456448 | tf_op jit(solution)/shard_map/all_gather | solution.py:40
  9.7 193.7 %all-gather.8.cloned.1.call-start = ((), (), s32[]{:S(2)}) async-start(), calls=%async_computation.9 | async-start | bytes 2228224 | tf_op jit(solution)/shard_map/all_gather | solution.py:99
  15.2 25.0 %all-to-all-start = ((bf16[16,16,1024]{2,1,0:T(8,128)(2,1)}), bf16[16,16,1024]{2,1,0:T(8,128)(2,1)S(1)}, u32[]{:S(2)}, u32[]{:S(2)}) async-start(bf16[16,16,1024]{2,1,0:T(8,128)(2,1)} %broadcast_select_fusion.2), calls=%async_computation | async-start | bytes 1048576 | tf_op jit(solution)/shard_map/all_to_all | solution.py:70
  40.9 55.7 %copy-start.6 = (bf16[16,16,1024]{2,1,0:T(8,128)(2,1)}, bf16[16,16,1024]{2,1,0:T(8,128)(2,1)S(1)}, u32[]{:S(2)}) copy-start(bf16[16,16,1024]{2,1,0:T(8,128)(2,1)S(1)} %broadcast_select_fusion.1) | copy-start | bytes 1572868
  98.1 5.3 %copy-start.11 = (bf16[256,256]{1,0:T(8,128)(2,1)S(1)}, bf16[256,256]{1,0:T(8,128)(2,1)}, u32[]{:S(2)}) copy-start(bf16[256,256]{1,0:T(8,128)(2,1)} %param.22) | copy-start | bytes 393220
  98.1 5.5 %copy-start.10 = (bf16[256,256]{1,0:T(8,128)(2,1)S(1)}, bf16[256,256]{1,0:T(8,128)(2,1)}, u32[]{:S(2)}) copy-start(bf16[256,256]{1,0:T(8,128)(2,1)} %param.25) | copy-start | bytes 393220
  98.1 7.6 %copy-start.7 = (bf16[16,16,1024]{2,1,0:T(8,128)(2,1)S(1)}, bf16[16,16,1024]{2,1,0:T(8,128)(2,1)}, u32[]{:S(2)}) copy-start(bf16[16,16,1024]{2,1,0:T(8,128)(2,1)} %copy-done.6) | copy-start | bytes 1572868
  98.1 60.2 %all-to-all-start.1 = ((bf16[8,256,512]{2,1,0:T(8,128)(2,1)}), bf16[8,256,512]{2,1,0:T(8,128)(2,1)}, u32[]{:S(2)}, u32[]{:S(2)}) async-start(bf16[8,256,512]{2,1,0:T(8,128)(2,1)} %bitcast.135), calls=%async_computation.1 | async-start | bytes 4194304 | tf_op jit(solution)/shard_map/all_to_all | solution.py:17
  102.7 215.0 %reduce-scatter.3.cloned.1.call-start = ((), (), s32[]{:S(2)}) async-start(), calls=%async_computation.7 | async-start | bytes 8912896 | tf_op jit(solution)/shard_map/reduce_scatter | solution.py:77
  160.3 1.7 copy-start.8
  161.9 41.4 %all-to-all-start.2 = ((bf16[8,256,512]{1,2,0:T(8,128)(2,1)}), bf16[8,256,512]{1,2,0:T(8,128)(2,1)S(1)}, u32[]{:S(2)}, u32[]{:S(2)}) async-start(bf16[8,256,512]{1,2,0:T(8,128)(2,1)} %broadcast_in_dim.101), calls=%async_computation.3 | async-start | bytes 4194304 | tf_op jit(solution)/shard_map/all_to_all | solution.py:29
  166.8 233.7 %reduce-scatter.5.cloned.1.call-start = ((), (), s32[]{:S(2)}) async-start(), calls=%async_computation.10 | async-start | bytes 4456448 | tf_op jit(solution)/shard_map/reduce_scatter | solution.py:54
  186.6 16.7 %copy-start.9 = (f32[256,256]{0,1:T(8,128)S(1)}, f32[256,256]{0,1:T(8,128)}, u32[]{:S(2)}) copy-start(f32[256,256]{0,1:T(8,128)} %copy.86) | copy-start | bytes 786436
  203.4 3.1 copy-start.2
  203.4 3.2 copy-start.4
  262.5 3.9 copy-start.5
  271.7 1.6 copy-start.3
  275.4 45.3 %all-to-all-start.3 = ((bf16[16,256,256]{1,2,0:T(8,128)(2,1)}), bf16[16,256,256]{1,2,0:T(8,128)(2,1)}, u32[]{:S(2)}, u32[]{:S(2)}) async-start(bf16[16,256,256]{1,2,0:T(8,128)(2,1)} %bitcast.134), calls=%async_computation.4 | async-start | bytes 4194304 | tf_op jit(solution)/shard_map/all_to_all | solution.py:17
  317.7 84.5 %copy-start.1 = (bf16[256,4096]{1,0:T(8,128)(2,1)S(1)}, bf16[256,4096]{1,0:T(8,128)(2,1)}, u32[]{:S(2)}) copy-start(bf16[256,4096]{1,0:T(8,128)(2,1)} %param.19) | copy-start | bytes 6291460
Sparse Core Ops, SparseCore 0:
  10.5 80.3 all-gather.3
  93.9 55.5 all-gather.5
  151.8 51.5 all-gather.7
  207.5 110.1 reduce-scatter.2
  321.5 78.9 reduce-scatter.4
where the time goes:
time: 411 us; the launch traced here: 409 us
  waiting for transfers between devices  234 us (57%)
  matrix products  66 us (16%)
  local copies, waits for them, and re-layouts  54.2 us (13%)
  starting transfers between devices  21.3 us (5%)
  other arithmetic  18.1 us (4%)
  between operations  14.7 us (4%)
    reduce_scatter x1, waiting for transfers between devices, sent_together(): lax.psum_scatter(both, axis, scatter_dimension=dim, tiled=True)  77.2 us
    all_gather x1, waiting for transfers between devices, body(): lax.all_gather(w_proj, 'seq', axis=0, tiled=True)  49.9 us
    all_gather x1, waiting for transfers between devices, in_one_piece(): lax.all_gather(both, axis, axis=dim, tiled=True)  38.1 us
    reduce_scatter x1, waiting for transfers between devices, body(): lax.psum_scatter(lax.dot_general(y_in, natural, (((0,), (0,)), ((), ())),...  37.9 us
    dynamic_slice x24, local copies, waits for them, and re-layouts, body(): lax.scan(statistics, start_stats, (key_blocks, pos_blocks))  20.8 us
    dot_general x16, matrix products, scores_of(): jnp.einsum('qhd,khd->hqk', query_heads, key_block, preferred_element_type...  20.8 us
    all_to_all x1, waiting for transfers between devices, body(): lax.all_to_all(outgoing, 'seq', split_axis=0, concat_axis=0, tiled=True)  16.4 us
    all_gather x1, waiting for transfers between devices, body(): lax.all_gather(w_out, 'seq', axis=1, tiled=True)  12.7 us
  transfers between devices with their start and end apart: 9, of which 6 were waited for; matrix products, arithmetic and copies ran while one was open for 33% of the time, Pallas kernels for 0%

commit v1 on v0

--- a/solution.py
+++ b/solution.py
@@ -5,6 +5,13 @@
 from jax.sharding import PartitionSpec as P
 
 HEAD_DIM = 128
+
+
+def gather_over(array, axis, dim):
+    peers = lax.axis_size(axis)
+    blocks = jnp.stack([array for _ in range(peers)])
+    blocks = lax.all_to_all(blocks, axis, split_axis=0, concat_axis=0)
+    return jnp.concatenate(blocks, axis=dim)
 
 
 def in_blocks(shard, dim, peers):
@@ -86,10 +93,7 @@
         .astype(half)
     )
     head_part = lax.dot_general(
-        natural,
-        lax.all_gather(w_proj, "seq", axis=0, tiled=True),
-        (((1,), (1,)), ((), ())),
-        preferred_element_type=flt,
+        natural, gather_over(w_proj, "seq", 0), (((1,), (1,)), ((), ())), preferred_element_type=flt
     )
     layer_grad = summed_on_arrival(head_part.astype(jnp.bfloat16), "head", 1).astype(half)
     full_grad = gathered_copies(layer_grad, "head", 1)

time: 411 us -> 388 us (0.944)
  waiting for transfers between devices: 234 us -> 197 us
  blocking collectives: 0 us -> 22.1 us
  local copies, waits for them, and re-layouts: 54.2 us -> 45.4 us
    all_to_all x1, waiting for transfers between devices: 16.4 us -> 106 us  [gather_over(): blocks = lax.all_to_all(blocks, axis, split_axis=0, concat_axis=0)]
    all_gather x1 -> x0, waiting for transfers between devices: 49.9 us -> none  [body(): lax.all_gather(w_proj, 'seq', axis=0, tiled=True)]
    reduce_scatter x1, waiting for transfers between devices: 77.2 us -> 38.5 us  [sent_together(): lax.psum_scatter(both, axis, scatter_dimension=dim, tiled=True)]
    all_gather x1, waiting for transfers between devices: 38.1 us -> 0.02 us  [in_one_piece(): lax.all_gather(both, axis, axis=dim, tiled=True)]
    reduce_scatter x1, waiting for transfers between devices: 37.9 us -> 0.01 us  [body(): lax.psum_scatter(lax.dot_general(y_in, natural, (((0,), (0,)), ((), ())),...]
    all_to_all x2, waiting for transfers between devices: 0.01 us -> 37.2 us  [summed_on_arrival(): lax.all_to_all(pieces, axis, split_axis=0, concat_axis=0, tiled=True)]
    all_to_all x0 -> x1, blocking collectives: none -> 22.1 us  [body(): lax.all_to_all(outgoing, 'seq', split_axis=0, concat_axis=0, tiled=True)]
    all_to_all x1, waiting for transfers between devices: 0.01 us -> 14.1 us  [from_everyone(): lax.all_to_all(jnp.broadcast_to(shard[None], (peers, *shard.shape)), axis...]
  transfers between devices with their start and end apart: 9 -> 8, of which waited for: 6 -> 5; matrix products, arithmetic and copies ran while one was open for 33% -> 33% of each run, Pallas kernels for 0% -> 0%
where the time goes in v1:
time: 388 us; the launch traced here: 386 us
  waiting for transfers between devices  197 us (51%)
  matrix products  67.4 us (17%)
  local copies, waits for them, and re-layouts  45.4 us (12%)
  blocking collectives  22.1 us (6%)
  starting transfers between devices  21.5 us (6%)
  other arithmetic  17.7 us (5%)
  between operations  14.7 us (4%)
    all_to_all x1, waiting for transfers between devices, gather_over(): blocks = lax.all_to_all(blocks, axis, split_axis=0, concat_axis=0)  106 us
    reduce_scatter x1, waiting for transfers between devices, sent_together(): lax.psum_scatter(both, axis, scatter_dimension=dim, tiled=True)  38.5 us
    all_to_all x2, waiting for transfers between devices, summed_on_arrival(): lax.all_to_all(pieces, axis, split_axis=0, concat_axis=0, tiled=True)  37.2 us
    all_to_all x1, blocking collectives, body(): lax.all_to_all(outgoing, 'seq', split_axis=0, concat_axis=0, tiled=True)  22.1 us
    dot_general x16, matrix products, scores_of(): jnp.einsum('qhd,khd->hqk', query_heads, key_block, preferred_element_type...  20.8 us
    all_to_all x1, waiting for transfers between devices, from_everyone(): lax.all_to_all(jnp.broadcast_to(shard[None], (peers, *shard.shape)), axis...  14.1 us
    all_to_all x2, starting transfers between devices, summed_on_arrival(): lax.all_to_all(pieces, axis, split_axis=0, concat_axis=0, tiled=True)  12 us
    dot_general x8, matrix products, backward(): jnp.einsum('hqk,khd->qhd', grad_scores, key_block, preferred_element_type...  10.1 us
  transfers between devices with their start and end apart: 8, of which 5 were waited for; matrix products, arithmetic and copies ran while one was open for 33% of the time, Pallas kernels for 0%

profile of v1, /device:TPU:0, one launch (start us, length us, event | category | flops | bytes accessed | tf_op | source)
XLA Modules:
  0.0 386.2 jit_solution(10437219438366620825)
XLA Ops:
  13.1 22.1 %all_to_all.25 = bf16[16,16,1024]{2,1,0:T(8,128)(2,1)S(1)} all-to-all(bf16[16,16,1024]{2,1,0:T(8,128)(2,1)S(1)} %broadcast_select_fusion.2), channel_id=1, replica_groups=mesh['seq'=16,'head'=8] {'seq'}, dimensions={0} | all-to-all | bytes 1048576 | tf_op jit(solution)/shard_map/all_to_all | solution.py:77
  35.2 4.3 %stack.2 = bf16[16,256,1024]{2,1,0:T(8,128)(2,1)} broadcast(bf16[256,1024]{1,0:T(8,128)(2,1)S(1)} %copy-done.7), dimensions={1,2} | broadcast | bytes 8912896 | tf_op jit(solution)/shard_map/stack | solution.py:12
  39.5 4.9 %all-to-all-start.1 = ((bf16[16,256,1024]{2,1,0:T(8,128)(2,1)}), bf16[16,256,1024]{2,1,0:T(8,128)(2,1)}, u32[]{:S(2)}, u32[]{:S(2)}) async-start(bf16[16,256,1024]{2,1,0:T(8,128)(2,1)} %stack.2), calls=%async_computation.1 | async-start | bytes 16777216 | tf_op jit(solution)/shard_map/all_to_all | solution.py:13
  47.9 106.0 %all-to-all-done.1 = bf16[16,256,1024]{2,1,0:T(8,128)(2,1)} async-done(((bf16[16,256,1024]{2,1,0:T(8,128)(2,1)}), bf16[16,256,1024]{2,1,0:T(8,128)(2,1)}, u32[]{:S(2)}, u32[]{:S(2)}) %all-to-all-start.1) | async-done | bytes 8388640 | tf_op jit(solution)/shard_map/all_to_all | solution.py:13
  153.8 5.8 %convolution_convert_fusion = bf16[256,4096]{1,0:T(8,128)(2,1)S(1)} fusion(bf16[256,1024]{1,0:T(8,128)(2,1)S(1)} %bitcast.137, bf16[4096,1024]{1,0:T(8,128)(2,1)} %bitcast.2), kind=kOutput, calls=%fused_computation.47 | convolution fusion | flops 2148532224 | bytes 11010048 | tf_op jit(solution)/shard_map/dot_general | solution.py:95
  161.1 5.5 %all-to-all-start.2 = ((bf16[8,256,512]{2,1,0:T(8,128)(2,1)}), bf16[8,256,512]{2,1,0:T(8,128)(2,1)}, u32[]{:S(2)}, u32[]{:S(2)}) async-start(bf16[8,256,512]{2,1,0:T(8,128)(2,1)} %bitcast.133), calls=%async_computation.2 | async-start | bytes 4194304 | tf_op jit(solution)/shard_map/all_to_all | solution.py:24
  169.0 5.6 %convert_bitcast_fusion = bf16[4096,1024]{0,1:T(8,128)(2,1)} fusion(bf16[256,1024]{1,0:T(8,128)(2,1)S(1)} %bitcast.138, bf16[256,4096]{1,0:T(8,128)(2,1)S(1)} %copy-done), kind=kOutput, calls=%fused_computation.46 | convolution fusion | flops 2151677952 | bytes 11010048 | tf_op jit(solution)/shard_map/dot_general | solution.py:85
  174.7 4.8 %fusion.40 = (bf16[4096,256]{1,0:T(8,128)(2,1)}, bf16[4096,256]{1,0:T(8,128)(2,1)}) fusion(bf16[4096,512]{1,0:T(8,128)(2,1)} %all-gather.3.cloned.1.call-done), kind=kLoop, calls=%fused_computation.99 | loop fusion | bytes 8388608 | tf_op jit(solution)/shard_map/slice | solution.py:49
  179.5 2.5 reshape.175
  183.9 10.6 %all-to-all-done.2 = bf16[8,256,512]{2,1,0:T(8,128)(2,1)} async-done(((bf16[8,256,512]{2,1,0:T(8,128)(2,1)}), bf16[8,256,512]{2,1,0:T(8,128)(2,1)}, u32[]{:S(2)}, u32[]{:S(2)}) %all-to-all-start.2) | async-done | bytes 2097184 | tf_op jit(solution)/shard_map/all_to_all | solution.py:24
  194.5 2.2 reduce_sum.80
  198.3 4.4 %all-to-all-start.3 = ((bf16[8,256,512]{1,2,0:T(8,128)(2,1)}), bf16[8,256,512]{1,2,0:T(8,128)(2,1)}, u32[]{:S(2)}, u32[]{:S(2)}) async-start(bf16[8,256,512]{1,2,0:T(8,128)(2,1)} %broadcast_in_dim.101), calls=%async_computation.4 | async-start | bytes 4194304 | tf_op jit(solution)/shard_map/all_to_all | solution.py:36
  202.9 14.0 %while.28 = (s32[]{:T(128)}, f32[2,256]{1,0:T(2,128)S(1)}, f32[2,256]{1,0:T(2,128)S(1)}, s32[8,512]{1,0:T(8,128)S(1)}, bf16[8,512,2,128]{3,1,2,0:T(8,128)(2,1)},...) while((s32[]{:T(128)}, f32[2,256]{1,0:T(2,128)S(1)}, ...), condition=%wide.region_12.14_spmd.clone, body=%wide.region_9.13_spmd.clone.sunk | while | flops 68815616 | bytes 2919024 | solution.py:160
  216.9 4.0 %reshape.176 = bf16[8,512,2,128]{3,2,1,0:T(2,128)(2,1)} reshape(bf16[4096,256]{1,0:T(8,128)(2,1)} %get-tuple-element.322) | data formatting | bytes 4194304 | tf_op jit(solution)/shard_map/reshape | solution.py:136
  221.0 14.1 %all-to-all-done.3 = bf16[8,256,512]{1,2,0:T(8,128)(2,1)} async-done(((bf16[8,256,512]{1,2,0:T(8,128)(2,1)}), bf16[8,256,512]{1,2,0:T(8,128)(2,1)}, u32[]{:S(2)}, u32[]{:S(2)}) %all-to-all-start.3) | async-done | bytes 2097184 | tf_op jit(solution)/shard_map/all_to_all | solution.py:36
  235.1 3.0 multiply_reduce_fusion
  238.2 49.8 %while.29 = (s32[]{:T(128)}, f32[256,2,128]{0,2,1:T(8,128)S(1)}, bf16[8,512,2,128]{3,1,2,0:T(8,128)(2,1)}, bf16[8,512,2,128]{3,1,2,0:T(8,128)(2,1)}, bf16[8,512,...) while((s32[]{:T(128)}, f32[256,2,128]{0,2,1:T(8,128)S(1)}, ...), condition=%wide.region_15.17_spmd.clone, body=%wide.region_14.16_spmd.clone.sunk | while | flops 337903872 | bytes 8403099 | solution.py:180
  288.0 3.9 %copy.75 = bf16[8,512,2,128]{3,2,1,0:T(2,128)(2,1)S(1)} copy(bf16[8,512,2,128]{3,1,2,0:T(8,128)(2,1)} %get-tuple-element.116) | data formatting | bytes 4194304 | tf_op jit(solution)/shard_map/convert_element_type | solution.py:189
  292.0 2.2 copy.76
  294.9 2.3 pad_maximum_fusion
  297.3 3.6 convolution_convert_fusion.1
  300.9 6.5 %all-to-all-start.4 = ((bf16[16,256,256]{1,2,0:T(8,128)(2,1)}), bf16[16,256,256]{1,2,0:T(8,128)(2,1)}, u32[]{:S(2)}, u32[]{:S(2)}) async-start(bf16[16,256,256]{1,2,0:T(8,128)(2,1)} %bitcast.9), calls=%async_computation.5 | async-start | bytes 4194304 | tf_op jit(solution)/shard_map/all_to_all | solution.py:24
  310.3 26.5 %all-to-all-done.4 = bf16[16,256,256]{1,2,0:T(8,128)(2,1)} async-done(((bf16[16,256,256]{1,2,0:T(8,128)(2,1)}), bf16[16,256,256]{1,2,0:T(8,128)(2,1)}, u32[]{:S(2)}, u32[]{:S(2)}) %all-to-all-start.4) | async-done | bytes 2097184 | tf_op jit(solution)/shard_map/all_to_all | solution.py:24
  339.5 38.5 %reduce-scatter.5.cloned.1.call-done = bf16[256,512]{1,0:T(8,128)(2,1)} async-done(((bf16[4096,512]{1,0:T(8,128)(2,1)}), bf16[256,512]{1,0:T(8,128)(2,1)}) %reduce-scatter.5.cloned.1.call-update) | async-done | bytes 262160 | tf_op jit(solution)/shard_map/reduce_scatter | solution.py:61
  (212 shorter events, 87.4 us)
Async XLA Ops:
  7.2 161.9 %copy-start = (bf16[256,4096]{1,0:T(8,128)(2,1)S(1)}, bf16[256,4096]{1,0:T(8,128)(2,1)}, u32[]{:S(2)}) copy-start(bf16[256,4096]{1,0:T(8,128)(2,1)} %param.19) | copy-start | bytes 6291460
  7.2 28.0 %copy-start.7 = (bf16[256,1024]{1,0:T(8,128)(2,1)S(1)}, bf16[256,1024]{1,0:T(8,128)(2,1)}, u32[]{:S(2)}) copy-start(bf16[256,1024]{1,0:T(8,128)(2,1)} %param.20) | copy-start | bytes 1572868
  7.2 167.5 %all-gather.3.cloned.1.call-start = ((), (), s32[]{:S(2)}) async-start(), calls=%async_computation.8 | async-start | bytes 4456448 | tf_op jit(solution)/shard_map/all_gather | solution.py:47
  39.5 6.9 %copy-start.9 = (s32[16]{0:T(128)S(1)}, s32[16]{0:T(128)}, u32[]{:S(2)}) copy-start(s32[16]{0:T(128)} %param.18) | copy-start | bytes 196
  39.5 114.4 %all-to-all-start.1 = ((bf16[16,256,1024]{2,1,0:T(8,128)(2,1)}), bf16[16,256,1024]{2,1,0:T(8,128)(2,1)}, u32[]{:S(2)}, u32[]{:S(2)}) async-start(bf16[16,256,1024]{2,1,0:T(8,128)(2,1)} %stack.2), calls=%async_computation.1 | async-start | bytes 16777216 | tf_op jit(solution)/shard_map/all_to_all | solution.py:13
  44.3 176.6 %all-gather.5.cloned.1.call-start = ((), (), s32[]{:S(2)}) async-start(), calls=%async_computation.9 | async-start | bytes 2228224 | tf_op jit(solution)/shard_map/all_gather | solution.py:103
  47.8 111.8 %copy-start.3 = (bf16[16,16,1024]{2,1,0:T(8,128)(2,1)}, bf16[16,16,1024]{2,1,0:T(8,128)(2,1)S(1)}, u32[]{:S(2)}) copy-start(bf16[16,16,1024]{2,1,0:T(8,128)(2,1)S(1)} %broadcast_select_fusion.1) | copy-start | bytes 1572868
  161.1 6.1 %copy-start.6 = (bf16[256,256]{1,0:T(8,128)(2,1)S(1)}, bf16[256,256]{1,0:T(8,128)(2,1)}, u32[]{:S(2)}) copy-start(bf16[256,256]{1,0:T(8,128)(2,1)} %param.25) | copy-start | bytes 393220
  161.1 6.3 %copy-start.8 = (bf16[256,256]{1,0:T(8,128)(2,1)S(1)}, bf16[256,256]{1,0:T(8,128)(2,1)}, u32[]{:S(2)}) copy-start(bf16[256,256]{1,0:T(8,128)(2,1)} %param.22) | copy-start | bytes 393220
  161.1 7.9 %copy-start.4 = (bf16[16,16,1024]{2,1,0:T(8,128)(2,1)S(1)}, bf16[16,16,1024]{2,1,0:T(8,128)(2,1)}, u32[]{:S(2)}) copy-start(bf16[16,16,1024]{2,1,0:T(8,128)(2,1)} %copy-done.3) | copy-start | bytes 1572868
  161.1 33.3 %all-to-all-start.2 = ((bf16[8,256,512]{2,1,0:T(8,128)(2,1)}), bf16[8,256,512]{2,1,0:T(8,128)(2,1)}, u32[]{:S(2)}, u32[]{:S(2)}) async-start(bf16[8,256,512]{2,1,0:T(8,128)(2,1)} %bitcast.133), calls=%async_computation.2 | async-start | bytes 4194304 | tf_op jit(solution)/shard_map/all_to_all | solution.py:24
  166.6 141.6 %reduce-scatter.3.cloned.1.call-start = ((), (), s32[]{:S(2)}) async-start(), calls=%async_computation.7 | async-start | bytes 8912896 | tf_op jit(solution)/shard_map/reduce_scatter | solution.py:84
  196.7 1.6 copy-start.5
  198.3 36.8 %all-to-all-start.3 = ((bf16[8,256,512]{1,2,0:T(8,128)(2,1)}), bf16[8,256,512]{1,2,0:T(8,128)(2,1)}, u32[]{:S(2)}, u32[]{:S(2)}) async-start(bf16[8,256,512]{1,2,0:T(8,128)(2,1)} %broadcast_in_dim.101), calls=%async_computation.4 | async-start | bytes 4194304 | tf_op jit(solution)/shard_map/all_to_all | solution.py:36
  202.7 175.3 %reduce-scatter.5.cloned.1.call-start = ((), (), s32[]{:S(2)}) async-start(), calls=%async_computation.10 | async-start | bytes 4456448 | tf_op jit(solution)/shard_map/reduce_scatter | solution.py:61
  288.0 3.9 %copy-start.2 = (bf16[8,512,2,128]{3,1,2,0:T(8,128)(2,1)S(1)}, bf16[8,512,2,128]{3,1,2,0:T(8,128)(2,1)}, u32[]{:S(2)}) copy-start(bf16[8,512,2,128]{3,1,2,0:T(8,128)(2,1)} %get-tuple-element.117) | copy-start | bytes 6291460
  300.9 35.9 %all-to-all-start.4 = ((bf16[16,256,256]{1,2,0:T(8,128)(2,1)}), bf16[16,256,256]{1,2,0:T(8,128)(2,1)}, u32[]{:S(2)}, u32[]{:S(2)}) async-start(bf16[16,256,256]{1,2,0:T(8,128)(2,1)} %bitcast.9), calls=%async_computation.5 | async-start | bytes 4194304 | tf_op jit(solution)/shard_map/all_to_all | solution.py:24
  307.4 72.2 %copy-start.1 = (bf16[256,4096]{1,0:T(8,128)(2,1)S(1)}, bf16[256,4096]{1,0:T(8,128)(2,1)}, u32[]{:S(2)}) copy-start(bf16[256,4096]{1,0:T(8,128)(2,1)} %param.19) | copy-start | bytes 6291460
Sparse Core Ops, SparseCore 0:
  11.0 110.3 all-gather.2
  123.8 59.5 all-gather.4
  187.7 104.0 reduce-scatter.2
  297.4 80.5 reduce-scatter.4
